TPU v7x, 32 devices: a whole 2x2x4 slice. The times are simulated.
32 devices in a mesh: blk: 8 (over z, y), rep: 4 (over x, core).
Axes of the slice: x: 2, y: 2, z: 4, core: 2. Of those that a mesh axis runs over, the one named last changes fastest.
Arguments:
- tokens: bfloat16 [4096, 8192], P(('blk', 'rep')), may hold values from -6 to 6
- gate_weight: bfloat16 [8, 8192], P('blk'), may hold values from -0.0625 to 0.0625
- up_weight: bfloat16 [8, 8192], P('blk'), may hold values from -0.0625 to 0.0625
- down_weight: bfloat16 [8, 8192], P('blk'), may hold values from -2 to 2
Outputs:
- grad_gate: float32 [8, 8192], P('blk')
- grad_up: float32 [8, 8192], P('blk')
- grad_down: float32 [8, 8192], P('blk')
All inputs are finite; a program needn't handle non-finite values.
Results may differ from a plain program's by a relative error of at most 0.0027.
Values may be sent and summed in bfloat16 or wider, within the bound.
A program may use at most 64 MiB of HBM per device.

v0:
```python
import jax
import jax.numpy as jnp
from jax import lax
from jax.sharding import PartitionSpec as P


def per_device(tokens, gate_weight, up_weight, down_weight):
    tok_rows = tokens.shape[0]
    features = tokens.shape[1]
    cycle_size = lax.axis_size("blk")
    group_size = lax.axis_size("rep")
    loss_scale = float(tok_rows * cycle_size * group_size) ** (-0.5)
    right_numbers = (((1,), (1,)), ((), ()))
    left_numbers = (((0,), (0,)), ((), ()))
    gate_piece = lax.all_gather(gate_weight, "blk", axis=0, tiled=True)
    up_piece = lax.all_gather(up_weight, "blk", axis=0, tiled=True)
    down_piece = lax.all_gather(down_weight, "blk", axis=0, tiled=True)
    gate_pre = lax.dot_general(
        tokens, gate_piece, right_numbers, preferred_element_type=jnp.float32
    )
    up_pre = lax.dot_general(tokens, up_piece, right_numbers, preferred_element_type=jnp.float32)
    hidden_piece = (gate_pre * jax.nn.sigmoid(gate_pre) * up_pre).astype(jnp.bfloat16)
    layer_out = jnp.dot(hidden_piece, down_piece, preferred_element_type=jnp.float32)
    gate_all = gate_pre
    up_all = up_pre
    gate_full = gate_piece
    up_full = up_piece
    down_full = down_piece
    carry = (layer_out, gate_all, up_all, hidden_piece, gate_full, up_full, down_full)
    layer_out, gate_pre, up_pre, hidden, gate_full, up_full, down_full = carry
    cotangent = (layer_out * loss_scale).astype(jnp.bfloat16)
    hidden_grad = lax.dot_general(
        cotangent, down_full, right_numbers, preferred_element_type=jnp.float32
    )
    sigmoid_gate = jax.nn.sigmoid(gate_pre)
    active = gate_pre * sigmoid_gate
    gate_grad = (
        hidden_grad * up_pre * (sigmoid_gate * (1.0 + gate_pre * (1.0 - sigmoid_gate)))
    ).astype(jnp.bfloat16)
    up_grad = (hidden_grad * active).astype(jnp.bfloat16)
    gate_term = lax.dot_general(gate_grad, tokens, left_numbers, preferred_element_type=jnp.float32)
    up_term = lax.dot_general(up_grad, tokens, left_numbers, preferred_element_type=jnp.float32)
    down_term = lax.dot_general(hidden, cotangent, left_numbers, preferred_element_type=jnp.float32)
    shares = lax.psum_scatter(
        jnp.concatenate([gate_term, up_term, down_term], axis=1),
        "blk",
        scatter_dimension=0,
        tiled=True,
    )
    totals = lax.psum(shares, "rep")
    return (totals[:, :features], totals[:, features : 2 * features], totals[:, 2 * features :])


def solution(mesh):
    in_specs = (P(("blk", "rep"), None), P("blk", None), P("blk", None), P("blk", None))
    out_specs = (P("blk", None), P("blk", None), P("blk", None))
    return jax.shard_map(
        per_device, mesh=mesh, in_specs=in_specs, out_specs=out_specs, check_vma=False
    )
```

profile of v0, /device:TPU:0, one launch (start us, length us, event | category | flops | bytes accessed | tf_op | source)
XLA Modules:
  0.0 225.2 jit_solution(10801026277273655064)
XLA Ops:
  7.2 0.0 copy-start
  7.2 0.0 all-reduce.6.cloned.1.call-start
  7.2 32.9 %all-gather.2 = bf16[8,1,8192]{2,1,0:T(2,128)(2,1)S(1)} all-gather(bf16[1,1,8192]{2,1,0:T(2,128)(2,1)} %bitcast.25), channel_id=1, replica_groups=mesh['blk'=8,'rep'=4] {'blk'}, dimensions={0}, use_global_device_ids=true | all-gather | bytes 147456 | tf_op jit(solution)/shard_map/all_gather | solution.py:17
  40.1 30.9 %all-gather = bf16[8,1,8192]{2,1,0:T(2,128)(2,1)S(1)} all-gather(bf16[1,1,8192]{2,1,0:T(2,128)(2,1)} %bitcast.26), channel_id=1, replica_groups=mesh['blk'=8,'rep'=4] {'blk'}, dimensions={0}, use_global_device_ids=true | all-gather | bytes 147456 | tf_op jit(solution)/shard_map/all_gather | solution.py:15
  71.1 30.9 %all-gather.1 = bf16[8,1,8192]{2,1,0:T(2,128)(2,1)S(1)} all-gather(bf16[1,1,8192]{2,1,0:T(2,128)(2,1)} %bitcast.27), channel_id=1, replica_groups=mesh['blk'=8,'rep'=4] {'blk'}, dimensions={0}, use_global_device_ids=true | all-gather | bytes 147456 | tf_op jit(solution)/shard_map/all_gather | solution.py:16
  102.0 0.0 copy-done
  102.0 0.7 fusion.7
  102.7 0.7 multiply_convert_fusion.2
  103.4 0.8 fusion
  104.1 0.6 fusion.1
  104.8 0.4 fusion.20
  105.2 0.4 fusion.14
  105.6 0.0 copy-start.1
  105.6 0.4 fusion.13
  106.0 1.0 pad_maximum_fusion
  106.9 0.0 all-reduce.6.cloned.1.call-update
  107.0 0.0 all-reduce.4.cloned.1.call-start
  107.0 0.0 copy-done.1
  107.0 0.6 dynamic-slice
  107.6 75.8 %all-reduce.6.cloned.1.call-done = f32[8,24576]{1,0:T(8,128)} async-done(((f32[8,24576]{1,0:T(8,128)}), f32[8,24576]{1,0:T(8,128)}) %all-reduce.6.cloned.1.call-update) | async-done | bytes 786448
  183.4 2.5 %constant_dynamic-slice_fusion = f32[1,24576]{1,0:T(1,128)} fusion(f32[8,24576]{1,0:T(8,128)} %all-reduce.6.cloned.1.call-done, u32[]{:T(128)} %bitcast.3), kind=kLoop, calls=%fused_computation.22 | loop fusion | bytes 196612
  185.9 0.0 all-reduce.4.cloned.1.call-update
  185.9 31.0 %all-reduce.4.cloned.1.call-done = f32[1,24576]{1,0:T(1,128)} async-done(((f32[1,24576]{1,0:T(1,128)}), f32[1,24576]{1,0:T(1,128)}) %all-reduce.4.cloned.1.call-update) | async-done | bytes 98320 | tf_op jit(solution)/shard_map/psum | solution.py:50
  216.9 1.4 fusion.19
Async XLA Ops:
  7.2 94.9 %copy-start = (bf16[128,8192]{1,0:T(8,128)(2,1)S(1)}, bf16[128,8192]{1,0:T(8,128)(2,1)}, u32[]{:S(2)}) copy-start(bf16[128,8192]{1,0:T(8,128)(2,1)} %param.4) | copy-start | bytes 6291460
  7.2 176.2 %all-reduce.6.cloned.1.call-start = ((), (), s32[]{:S(2)}) async-start(), calls=%async_computation.1 | async-start | bytes 1572864
  105.6 1.4 copy-start.1
  107.0 109.9 %all-reduce.4.cloned.1.call-start = ((), (), s32[]{:S(2)}) async-start(), calls=%async_computation | async-start | bytes 196608 | tf_op jit(solution)/shard_map/psum | solution.py:50
Sparse Core Ops, SparseCore 0:
  107.1 76.2 all-reduce.5
  186.0 30.8 all-reduce.3
where the time goes:
time: 225 us
  waiting for transfers between devices  107 us (48%)
  blocking collectives  94.8 us (42%)
  between operations  14.1 us (6%)
  local copies, waits for them, and re-layouts  4.51 us (2%)
  matrix products  3.94 us (2%)
    unnamed x3, waiting for transfers between devices  75.8 us
    all_gather x1, blocking collectives, per_device(): down_piece = lax.all_gather(down_weight, 'blk', axis=0, tiled=True)  32.9 us
    psum x1, waiting for transfers between devices, per_device(): totals = lax.psum(shares, 'rep')  31 us
    all_gather x1, blocking collectives, per_device(): gate_piece = lax.all_gather(gate_weight, 'blk', axis=0, tiled=True)  30.9 us
    all_gather x1, blocking collectives, per_device(): up_piece = lax.all_gather(up_weight, 'blk', axis=0, tiled=True)  30.9 us
  transfers between devices with their start and end apart: 2, of which 2 were waited for; matrix products, arithmetic and copies ran while one was open for 0% of the time, Pallas kernels for 0%

commit v1 on v0

--- a/solution.py
+++ b/solution.py
@@ -2,6 +2,14 @@
 import jax.numpy as jnp
 from jax import lax
 from jax.sharding import PartitionSpec as P
+
+
+def added_up(x, axis):
+    n_dev, result = (lax.axis_size(axis), x)
+    for reach in [1 << k for k in range(n_dev.bit_length() - 1)]:
+        swap = [(i, i ^ reach) for i in range(n_dev)]
+        result = result + lax.ppermute(result, axis, swap)
+    return result
 
 
 def per_device(tokens, gate_weight, up_weight, down_weight):
@@ -47,7 +55,7 @@
         scatter_dimension=0,
         tiled=True,
     )
-    totals = lax.psum(shares, "rep")
+    totals = added_up(shares, "rep")
     return (totals[:, :features], totals[:, features : 2 * features], totals[:, 2 * features :])
 
 

time: 225 us -> 201 us (0.89)
  waiting for transfers between devices: 107 us -> 80.6 us
    psum x1 -> x0, waiting for transfers between devices: 31 us -> none  [per_device(): totals = lax.psum(shares, 'rep')]
    ppermute x0 -> x2, waiting for transfers between devices: none -> 4.67 us  [added_up(): result = result + lax.ppermute(result, axis, swap)]
    unnamed x3 -> x2, waiting for transfers between devices: 75.8 us -> 75.9 us
  transfers between devices with their start and end apart: 2 -> 3, of which waited for: 2 -> 3; matrix products, arithmetic and copies ran while one was open for 0% -> 0% of each run, Pallas kernels for 0% -> 0%
where the time goes in v1:
time: 201 us
  blocking collectives  94.8 us (47%)
  waiting for transfers between devices  80.6 us (40%)
  between operations  14.1 us (7%)
  matrix products  3.94 us (2%)
  local copies, waits for them, and re-layouts  3.09 us (2%)
  other arithmetic  2.95 us (1%)
    unnamed x2, waiting for transfers between devices  75.9 us
    all_gather x1, blocking collectives, per_device(): down_piece = lax.all_gather(down_weight, 'blk', axis=0, tiled=True)  32.9 us
    all_gather x1, blocking collectives, per_device(): gate_piece = lax.all_gather(gate_weight, 'blk', axis=0, tiled=True)  30.9 us
    all_gather x1, blocking collectives, per_device(): up_piece = lax.all_gather(up_weight, 'blk', axis=0, tiled=True)  30.9 us
    ppermute x2, waiting for transfers between devices, added_up(): result = result + lax.ppermute(result, axis, swap)  4.67 us
  transfers between devices with their start and end apart: 3, of which 3 were waited for; matrix products, arithmetic and copies ran while one was open for 0% of the time, Pallas kernels for 0%

profile of v1, /device:TPU:0, one launch (start us, length us, event | category | flops | bytes accessed | tf_op | source)
XLA Modules:
  0.0 201.0 jit_solution(495450403646162340)
XLA Ops:
  7.2 0.0 copy-start
  7.2 0.0 all-reduce.3.cloned.1.call-start
  7.2 32.9 %all-gather.2 = bf16[8,1,8192]{2,1,0:T(2,128)(2,1)S(1)} all-gather(bf16[1,1,8192]{2,1,0:T(2,128)(2,1)} %bitcast.25), channel_id=1, replica_groups=mesh['blk'=8,'rep'=4] {'blk'}, dimensions={0}, use_global_device_ids=true | all-gather | bytes 147456 | tf_op jit(solution)/shard_map/all_gather | solution.py:25
  40.1 30.9 %all-gather = bf16[8,1,8192]{2,1,0:T(2,128)(2,1)S(1)} all-gather(bf16[1,1,8192]{2,1,0:T(2,128)(2,1)} %bitcast.26), channel_id=1, replica_groups=mesh['blk'=8,'rep'=4] {'blk'}, dimensions={0}, use_global_device_ids=true | all-gather | bytes 147456 | tf_op jit(solution)/shard_map/all_gather | solution.py:23
  71.1 30.9 %all-gather.1 = bf16[8,1,8192]{2,1,0:T(2,128)(2,1)S(1)} all-gather(bf16[1,1,8192]{2,1,0:T(2,128)(2,1)} %bitcast.27), channel_id=1, replica_groups=mesh['blk'=8,'rep'=4] {'blk'}, dimensions={0}, use_global_device_ids=true | all-gather | bytes 147456 | tf_op jit(solution)/shard_map/all_gather | solution.py:24
  102.0 0.7 fusion.7
  102.7 0.7 multiply_convert_fusion.2
  103.4 0.8 fusion
  104.1 0.6 fusion.1
  104.8 0.4 fusion.20
  105.2 0.4 fusion.14
  105.6 0.4 fusion.13
  106.0 0.9 pad_maximum_fusion
  106.9 0.0 all-reduce.3.cloned.1.call-update
  107.0 0.6 dynamic-slice
  107.5 75.9 %all-reduce.3.cloned.1.call-done = f32[8,24576]{1,0:T(8,128)} async-done(((f32[8,24576]{1,0:T(8,128)}), f32[8,24576]{1,0:T(8,128)}) %all-reduce.3.cloned.1.call-update) | async-done | bytes 786448
  183.4 1.8 constant_dynamic-slice_fusion
  185.3 0.1 collective-permute-start
  185.3 1.3 collective-permute-done
  186.6 1.9 fusion.29
  188.5 1.5 collective-permute-start.1
  190.1 3.4 %collective-permute-done.1 = f32[1,24576]{1,0:T(1,128)S(1)} collective-permute-done((f32[1,24576]{1,0:T(1,128)S(1)}, f32[1,24576]{1,0:T(1,128)S(1)}, u32[]{:S(2)}, u32[]{:S(2)}) %collective-permute-start.1) | collective-permute-done | bytes 98336 | tf_op jit(solution)/shard_map/ppermute | solution.py:11
  193.5 0.1 add.18
  193.6 0.6 fusion.19
  (3 shorter events, 0.0 us)
Async XLA Ops:
  7.2 94.9 %copy-start = (bf16[128,8192]{1,0:T(8,128)(2,1)S(1)}, bf16[128,8192]{1,0:T(8,128)(2,1)}, u32[]{:S(2)}) copy-start(bf16[128,8192]{1,0:T(8,128)(2,1)} %param.4) | copy-start | bytes 6291460
  7.2 176.2 %all-reduce.3.cloned.1.call-start = ((), (), s32[]{:S(2)}) async-start(), calls=%async_computation | async-start | bytes 1572864
  105.6 1.4 copy-start.1
  185.3 1.4 collective-permute-start
  188.5 4.9 %collective-permute-start.1 = (f32[1,24576]{1,0:T(1,128)S(1)}, f32[1,24576]{1,0:T(1,128)S(1)}, u32[]{:S(2)}, u32[]{:S(2)}) collective-permute-start(f32[1,24576]{1,0:T(1,128)S(1)} %fusion.29), channel_id=1, source_target_pairs={{0,2},{1,3},{2,0},{3,1},{4,6},{5,7},{6,4},{7,5},{8,10},{9,11},{10,... | collective-permute-start | bytes 294920 | tf_op jit(solution)/shard_map/ppermute | solution.py:11
Sparse Core Ops, SparseCore 0:
  107.1 76.2 all-reduce.2
